TPU v7x, 32 devices: a whole 2x2x4 slice. The times are simulated.
32 devices in a mesh: py: 4 (over x, core), px: 8 (over z, y).
Axes of the slice: x: 2, y: 2, z: 4, core: 2. Of those that a mesh axis runs over, the one named last changes fastest.
Arguments:
- source_terms: float32 [256, 1024, 256], P('py', 'px'), may hold values from -6 to 6
- initial_values: float32 [256, 1024, 256], P('py', 'px'), may hold values from -6 to 6
- absorption: float32 [256, 1024, 256], P('py', 'px'), may hold values from 0.1 to 0.9
Outputs:
- solution: float32 [256, 1024, 256], P('py', 'px')
- remaining: float32 [256, 1024, 256], P('py', 'px')
All inputs are finite; a program needn't handle non-finite values.
Results may differ from a plain program's by a relative error of at most 0.000033.
Values sent between devices are 32-bit elements; how exact they have to be, the bound alone decides.
A program may use at most 128 MiB of HBM per device.

v0:
```python
import functools

import jax
import jax.numpy as jnp
from jax import lax
from jax.experimental import pallas as pl
from jax.experimental.pallas import tpu as pltpu
from jax.sharding import PartitionSpec as P

INNER = 9
LANES = 128
PAD = 8
MESH = pl.DeviceIdType.MESH


def kernel(
    sizes, load_in, start_in, mass_in, solution_out, remaining_out,
    one, two, load, mass, rate, coarse_one, coarse_two, coarse_load, coarse_rate,
    pair, side_send, side_recv, in_sem, out_sem, send_sem, recv_sem,
):
    chunks, ny, nx, count_y, count_x = sizes
    cy, cx = ny // 2, nx // 2
    my_y, my_x = lax.axis_index("py"), lax.axis_index("px")
    targets = (
        {"py": lax.rem(my_y + count_y - 1, count_y)},
        {"py": lax.rem(my_y + 1, count_y)},
        {"px": lax.rem(my_x + count_x - 1, count_x)},
        {"px": lax.rem(my_x + 1, count_x)},
    )

    def fetch(c, kind):
        part = pl.ds(c * LANES, LANES)
        if kind == 0:
            source, target = start_in, one.at[c, pl.ds(1, ny), pl.ds(PAD, nx), :]
        elif kind == 1:
            source, target = mass_in, mass.at[c]
        else:
            source, target = load_in, load.at[c]
        return pltpu.make_async_copy(source.at[:, :, part], target, in_sem.at[c, kind])

    def put(c, kind):
        source, target = ((one, solution_out), (two, remaining_out))[kind]
        return pltpu.make_async_copy(
            source.at[c, pl.ds(1, ny), pl.ds(PAD, nx), :],
            target.at[:, :, pl.ds(c * LANES, LANES)],
            out_sem.at[c, kind],
        )

    def copies(cells, c, turn, rows, columns):
        ends = (
            (cells.at[c, 1, pl.ds(PAD, columns), :], cells.at[c, rows + 1, pl.ds(PAD, columns), :]),
            (cells.at[c, rows, pl.ds(PAD, columns), :], cells.at[c, 0, pl.ds(PAD, columns), :]),
            (side_send.at[turn, c, 0, pl.ds(0, rows), :], side_recv.at[turn, c, 1, pl.ds(0, rows), :]),
            (side_send.at[turn, c, 1, pl.ds(0, rows), :], side_recv.at[turn, c, 0, pl.ds(0, rows), :]),
        )
        return [
            pltpu.make_async_remote_copy(
                src_ref=source,
                dst_ref=target,
                send_sem=send_sem.at[turn, c, way],
                recv_sem=recv_sem.at[turn, c, way],
                device_id=targets[way],
                device_id_type=MESH,
            )
            for way, (source, target) in enumerate(ends)
        ]

    def send(*where):
        for copy in copies(*where):
            copy.start()

    def receive(cells, c, turn, rows, columns):
        for copy in copies(cells, c, turn, rows, columns):
            copy.wait()

        def place(y, carry):
            cells[c, y + 1, pl.ds(PAD - 1, 1), :] = side_recv[turn, c, 0, pl.ds(y, 1), :]
            cells[c, y + 1, pl.ds(PAD + columns, 1), :] = side_recv[turn, c, 1, pl.ds(y, 1), :]
            return carry

        lax.fori_loop(0, rows, place, 0, unroll=8)

    def blocks(columns):
        size = min(columns, 64)
        return [(at, size) for at in range(0, columns, size)]

    def around(cells, c, y, at, size):
        return (
            (cells[c, y, pl.ds(PAD + at, size), :] + cells[c, y + 2, pl.ds(PAD + at, size), :])
            + cells[c, y + 1, pl.ds(PAD + at - 1, size), :]
        ) + cells[c, y + 1, pl.ds(PAD + at + 1, size), :]

    def keep(source, target, c, turn, y, at, size, columns, new):
        target[c, y + 1, pl.ds(PAD + at, size), :] = new
        if at == 0:
            side_send[turn, c, 0, pl.ds(y, 1), :] = new[0:1, :]
        if at + size == columns:
            side_send[turn, c, 1, pl.ds(y, 1), :] = new[size - 1 : size, :]

    def fine_sweep(source, target, c, turn, first):
        def row(y, carry):
            for at, size in blocks(nx):
                if first:
                    speed = 0.8 / (4.0 + mass[c, y, pl.ds(at, size), :])
                    rate[c, y, pl.ds(at, size), :] = speed
                else:
                    speed = rate[c, y, pl.ds(at, size), :]
                total = load[c, y, pl.ds(at, size), :] + around(source, c, y, at, size)
                new = 0.2 * source[c, y + 1, pl.ds(PAD + at, size), :] + speed * total
                keep(source, target, c, turn, y, at, size, nx, new)
            return carry

        lax.fori_loop(0, ny, row, 0)

    def coarse_sweep(source, target, c, turn):
        def row(y, carry):
            for at, size in blocks(cx):
                total = coarse_load[c, y, pl.ds(at, size), :] + around(source, c, y, at, size)
                new = (
                    0.2 * source[c, y + 1, pl.ds(PAD + at, size), :]
                    + coarse_rate[c, y, pl.ds(at, size), :] * total
                )
                keep(source, target, c, turn, y, at, size, cx, new)
            return carry

        lax.fori_loop(0, cy, row, 0)

    def defect(cells, c, y, at, size):
        return (load[c, y, pl.ds(at, size), :] + around(cells, c, y, at, size)) - (
            4.0 + mass[c, y, pl.ds(at, size), :]
        ) * cells[c, y + 1, pl.ds(PAD + at, size), :]

    def restrict(cells, c, turn):
        def row(y, carry):
            for at, size in blocks(nx):
                pair[0, pl.ds(at, size), :] = defect(cells, c, 2 * y, at, size) + defect(
                    cells, c, 2 * y + 1, at, size
                )
                pair[1, pl.ds(at, size), :] = (
                    mass[c, 2 * y, pl.ds(at, size), :] + mass[c, 2 * y + 1, pl.ds(at, size), :]
                )
            here = 0.5 * (pair[0, pl.ds(0, cx, stride=2), :] + pair[0, pl.ds(1, cx, stride=2), :])
            zero_order = 0.5 * (
                pair[1, pl.ds(0, cx, stride=2), :] + pair[1, pl.ds(1, cx, stride=2), :]
            )
            speed = 0.8 / (4.0 + zero_order)
            coarse_load[c, y] = here
            coarse_rate[c, y] = speed
            keep(None, coarse_one, c, turn, y, 0, cx, cx, speed * here)
            return carry

        lax.fori_loop(0, cy, row, 0)

    def correct_row(c, fine_row, coarse_row):
        extra = coarse_one[c, coarse_row, pl.ds(PAD, cx), :]
        for shift in range(2):
            spot = pl.ds(PAD + shift, cx, stride=2)
            one[c, fine_row, spot, :] = one[c, fine_row, spot, :] + extra

    def correct(c):
        correct_row(c, 0, 0)
        correct_row(c, ny + 1, cy + 1)

        def row(y, carry):
            for half in range(2):
                fine_row = 2 * y + 1 + half
                correct_row(c, fine_row, y + 1)
                for here, there in ((PAD - 1, PAD - 1), (PAD + nx, PAD + cx)):
                    one[c, fine_row, pl.ds(here, 1), :] = (
                        one[c, fine_row, pl.ds(here, 1), :]
                        + coarse_one[c, y + 1, pl.ds(there, 1), :]
                    )
            return carry

        lax.fori_loop(0, cy, row, 0)

    every = range(chunks)
    for c in every:
        for kind in range(3):
            fetch(c, kind).start()

    barrier = pltpu.get_barrier_semaphore()
    for target in targets:
        pl.semaphore_signal(barrier, inc=1, device_id=target, device_id_type=MESH)
    pl.semaphore_wait(barrier, 4)

    for c in every:
        fetch(c, 0).wait()

        def sides(y, carry):
            side_send[0, c, 0, pl.ds(y, 1), :] = one[c, y + 1, pl.ds(PAD, 1), :]
            side_send[0, c, 1, pl.ds(y, 1), :] = one[c, y + 1, pl.ds(PAD + nx - 1, 1), :]
            return carry

        lax.fori_loop(0, ny, sides, 0, unroll=8)
        send(one, c, 0, ny, nx)
    for c in every:
        fetch(c, 1).wait()
        fetch(c, 2).wait()
        receive(one, c, 0, ny, nx)
        fine_sweep(one, two, c, 1, True)
        send(two, c, 1, ny, nx)
    for c in every:
        receive(two, c, 1, ny, nx)
        fine_sweep(two, one, c, 0, False)
        send(one, c, 0, ny, nx)
    for c in every:
        receive(one, c, 0, ny, nx)
        restrict(one, c, 1)
        send(coarse_one, c, 1, cy, cx)

    def couple(step, carry):
        for c in every:
            receive(coarse_one, c, 1, cy, cx)
            coarse_sweep(coarse_one, coarse_two, c, 0)
            send(coarse_two, c, 0, cy, cx)
        for c in every:
            receive(coarse_two, c, 0, cy, cx)
            coarse_sweep(coarse_two, coarse_one, c, 1)
            send(coarse_one, c, 1, cy, cx)
        return carry

    lax.fori_loop(0, (INNER - 1) // 2, couple, 0)
    for c in every:
        receive(coarse_one, c, 1, cy, cx)
        correct(c)
        fine_sweep(one, two, c, 0, False)
        send(two, c, 0, ny, nx)
    for c in every:
        receive(two, c, 0, ny, nx)
        fine_sweep(two, one, c, 1, False)
        send(one, c, 1, ny, nx)
        put(c, 0).start()

    for c in every:
        receive(one, c, 1, ny, nx)

        def row(y, carry):
            for at, size in blocks(nx):
                two[c, y + 1, pl.ds(PAD + at, size), :] = defect(one, c, y, at, size)
            return carry

        lax.fori_loop(0, ny, row, 0)
        put(c, 1).start()
    for c in every:
        for kind in range(2):
            put(c, kind).wait()


def local(count_y, count_x, source_terms, initial_values, absorption):
    ny, nx, layers = source_terms.shape
    chunks = layers // LANES
    cy, cx = ny // 2, nx // 2
    kind = jnp.float32
    fine = pltpu.VMEM((chunks, ny, nx, LANES), kind)
    wide = pltpu.VMEM((chunks, ny + 2, nx + 2 * PAD, LANES), kind)
    coarse = pltpu.VMEM((chunks, cy, cx, LANES), kind)
    coarse_wide = pltpu.VMEM((chunks, cy + 2, cx + 2 * PAD, LANES), kind)
    side = pltpu.VMEM((2, chunks, 2, ny, LANES), kind)
    out = jax.ShapeDtypeStruct(source_terms.shape, kind)
    return pl.pallas_call(
        functools.partial(kernel, (chunks, ny, nx, count_y, count_x)),
        out_shape=(out, out),
        in_specs=[pl.BlockSpec(memory_space=pl.ANY)] * 3,
        out_specs=[pl.BlockSpec(memory_space=pl.ANY)] * 2,
        scratch_shapes=[
            wide, wide, fine, fine, fine, coarse_wide, coarse_wide, coarse, coarse,
            pltpu.VMEM((2, nx, LANES), kind), side, side,
            pltpu.SemaphoreType.DMA((chunks, 3)),
            pltpu.SemaphoreType.DMA((chunks, 2)),
            pltpu.SemaphoreType.DMA((2, chunks, 4)),
            pltpu.SemaphoreType.DMA((2, chunks, 4)),
        ],
        compiler_params=pltpu.CompilerParams(
            collective_id=0, has_side_effects=True, vmem_limit_bytes=66_000_000
        ),
    )(source_terms, initial_values, absorption)


def solution(mesh):
    spec = P("py", "px", None)
    return jax.shard_map(
        functools.partial(local, mesh.shape["py"], mesh.shape["px"]),
        mesh=mesh,
        in_specs=(spec, spec, spec),
        out_specs=(spec, spec),
        check_vma=False,
    )
```

profile of v0, /device:TPU:0, one launch (start us, length us, event | category | flops | bytes accessed | tf_op | source)
XLA Modules:
  0.0 99.9 jit_solution(15440876089546412600)
XLA Ops:
  0.6 88.0 %shard_map.50 = (f32[64,128,256]{2,1,0:T(8,128)}, f32[64,128,256]{2,1,0:T(8,128)}) custom-call(f32[64,128,256]{2,1,0:T(8,128)} %load_in.1, f32[64,128,256]{2,1,0:T(8,128)} %start_in.1, f32[64,128,256]{2,1,0:T(8,128)} %mass_in.1), custom_call_target="tpu_custom_call" | custom-call | tf_op jit(solution)/shard_map/pallas_call | solution.py:261
  88.6 0.0 copy-start
  88.6 7.9 %copy.7 = f32[64,128,256]{2,1,0:T(8,128)} copy(f32[64,128,256]{2,1,0:T(8,128)} %get-tuple-element.4) | data formatting | bytes 16777216
  96.5 0.0 copy-done
  96.5 3.4 %copy.8 = f32[64,128,256]{2,1,0:T(8,128)} copy(f32[64,128,256]{2,1,0:T(8,128)S(1)} %copy-done) | data formatting | bytes 16777216
Async XLA Ops:
  88.6 7.9 %copy-start = (f32[64,128,256]{2,1,0:T(8,128)S(1)}, f32[64,128,256]{2,1,0:T(8,128)}, u32[]{:S(2)}) copy-start(f32[64,128,256]{2,1,0:T(8,128)} %get-tuple-element.5) | copy-start | bytes 25165828
where the time goes:
time: 100 us; the launch traced here: 99.9 us
  Pallas kernels  88 us (88%)
  local copies, waits for them, and re-layouts  11.3 us (11%)
    pallas_call x1, Pallas kernels, local(): pl.pallas_call(functools.partial(kernel, (chunks, ny, nx, count_y, count_...  88 us
    unnamed x4, local copies, waits for them, and re-layouts  11.3 us

commit v1 on v0

--- a/solution.py
+++ b/solution.py
@@ -90,40 +90,47 @@
             + cells[c, y + 1, pl.ds(PAD + at - 1, size), :]
         ) + cells[c, y + 1, pl.ds(PAD + at + 1, size), :]
 
-    def keep(source, target, c, turn, y, at, size, columns, new):
+    def keep(target, c, y, at, size, new):
         target[c, y + 1, pl.ds(PAD + at, size), :] = new
-        if at == 0:
-            side_send[turn, c, 0, pl.ds(y, 1), :] = new[0:1, :]
-        if at + size == columns:
-            side_send[turn, c, 1, pl.ds(y, 1), :] = new[size - 1 : size, :]
+
+    def sweep(target, c, turn, rows, columns, value):
+        def row(y, carry):
+            for at, size in blocks(columns):
+                keep(target, c, y, at, size, value(y, at, size))
+            return carry
+
+        def sides(y, carry):
+            side_send[turn, c, 0, pl.ds(y, 1), :] = value(y, 0, PAD)[0:1, :]
+            side_send[turn, c, 1, pl.ds(y, 1), :] = value(y, columns - PAD, PAD)[PAD - 1 : PAD, :]
+            return carry
+
+        row(0, 0)
+        row(rows - 1, 0)
+        lax.fori_loop(0, rows, sides, 0, unroll=8)
+        send(target, c, turn, rows, columns)
+        lax.fori_loop(1, rows - 1, row, 0, unroll=2)
 
     def fine_sweep(source, target, c, turn, first):
-        def row(y, carry):
-            for at, size in blocks(nx):
-                if first:
-                    speed = 0.8 / (4.0 + mass[c, y, pl.ds(at, size), :])
-                    rate[c, y, pl.ds(at, size), :] = speed
-                else:
-                    speed = rate[c, y, pl.ds(at, size), :]
-                total = load[c, y, pl.ds(at, size), :] + around(source, c, y, at, size)
-                new = 0.2 * source[c, y + 1, pl.ds(PAD + at, size), :] + speed * total
-                keep(source, target, c, turn, y, at, size, nx, new)
-            return carry
-
-        lax.fori_loop(0, ny, row, 0)
+        def value(y, at, size):
+            if first:
+                speed = 0.8 / (4.0 + mass[c, y, pl.ds(at, size), :])
+                rate[c, y, pl.ds(at, size), :] = speed
+            else:
+                speed = rate[c, y, pl.ds(at, size), :]
+            total = load[c, y, pl.ds(at, size), :] + around(source, c, y, at, size)
+            return 0.2 * source[c, y + 1, pl.ds(PAD + at, size), :] + speed * total
+
+        sweep(target, c, turn, ny, nx, value)
 
     def coarse_sweep(source, target, c, turn):
-        def row(y, carry):
-            for at, size in blocks(cx):
-                total = coarse_load[c, y, pl.ds(at, size), :] + around(source, c, y, at, size)
-                new = (
-                    0.2 * source[c, y + 1, pl.ds(PAD + at, size), :]
-                    + coarse_rate[c, y, pl.ds(at, size), :] * total
-                )
-                keep(source, target, c, turn, y, at, size, cx, new)
-            return carry
-
-        lax.fori_loop(0, cy, row, 0)
+        def value(y, at, size):
+            total = coarse_load[c, y, pl.ds(at, size), :] + around(source, c, y, at, size)
+            return (
+                0.2 * source[c, y + 1, pl.ds(PAD + at, size), :]
+                + coarse_rate[c, y, pl.ds(at, size), :] * total
+            )
+
+        sweep(target, c, turn, cy, cx, value)
 
     def defect(cells, c, y, at, size):
         return (load[c, y, pl.ds(at, size), :] + around(cells, c, y, at, size)) - (
@@ -146,10 +153,13 @@
             speed = 0.8 / (4.0 + zero_order)
             coarse_load[c, y] = here
             coarse_rate[c, y] = speed
-            keep(None, coarse_one, c, turn, y, 0, cx, cx, speed * here)
-            return carry
-
-        lax.fori_loop(0, cy, row, 0)
+            new = speed * here
+            keep(coarse_one, c, y, 0, cx, new)
+            side_send[turn, c, 0, pl.ds(y, 1), :] = new[0:1, :]
+            side_send[turn, c, 1, pl.ds(y, 1), :] = new[cx - 1 : cx, :]
+            return carry
+
+        lax.fori_loop(0, cy, row, 0, unroll=4)
 
     def correct_row(c, fine_row, coarse_row):
         extra = coarse_one[c, coarse_row, pl.ds(PAD, cx), :]
@@ -172,7 +182,7 @@
                     )
             return carry
 
-        lax.fori_loop(0, cy, row, 0)
+        lax.fori_loop(0, cy, row, 0, unroll=4)
 
     every = range(chunks)
     for c in every:
@@ -199,11 +209,9 @@
         fetch(c, 2).wait()
         receive(one, c, 0, ny, nx)
         fine_sweep(one, two, c, 1, True)
-        send(two, c, 1, ny, nx)
     for c in every:
         receive(two, c, 1, ny, nx)
         fine_sweep(two, one, c, 0, False)
-        send(one, c, 0, ny, nx)
     for c in every:
         receive(one, c, 0, ny, nx)
         restrict(one, c, 1)
@@ -213,11 +221,9 @@
         for c in every:
             receive(coarse_one, c, 1, cy, cx)
             coarse_sweep(coarse_one, coarse_two, c, 0)
-            send(coarse_two, c, 0, cy, cx)
         for c in every:
             receive(coarse_two, c, 0, cy, cx)
             coarse_sweep(coarse_two, coarse_one, c, 1)
-            send(coarse_one, c, 1, cy, cx)
         return carry
 
     lax.fori_loop(0, (INNER - 1) // 2, couple, 0)
@@ -225,11 +231,9 @@
         receive(coarse_one, c, 1, cy, cx)
         correct(c)
         fine_sweep(one, two, c, 0, False)
-        send(two, c, 0, ny, nx)
     for c in every:
         receive(two, c, 0, ny, nx)
         fine_sweep(two, one, c, 1, False)
-        send(one, c, 1, ny, nx)
         put(c, 0).start()
 
     for c in every:
@@ -240,7 +244,7 @@
                 two[c, y + 1, pl.ds(PAD + at, size), :] = defect(one, c, y, at, size)
             return carry
 
-        lax.fori_loop(0, ny, row, 0)
+        lax.fori_loop(0, ny, row, 0, unroll=4)
         put(c, 1).start()
     for c in every:
         for kind in range(2):

time: 100 us -> 89 us (0.89)
  Pallas kernels: 88 us -> 76.9 us
    pallas_call x1, Pallas kernels: 88 us -> 76.9 us  [local(): pl.pallas_call(functools.partial(kernel, (chunks, ny, nx, count_y, count_...]
where the time goes in v1:
time: 89 us; the launch traced here: 88.8 us
  Pallas kernels  76.9 us (86%)
  local copies, waits for them, and re-layouts  11.3 us (13%)
    pallas_call x1, Pallas kernels, local(): pl.pallas_call(functools.partial(kernel, (chunks, ny, nx, count_y, count_...  76.9 us
    unnamed x4, local copies, waits for them, and re-layouts  11.3 us

profile of v1, /device:TPU:0, one launch (start us, length us, event | category | flops | bytes accessed | tf_op | source)
XLA Modules:
  0.0 88.8 jit_solution(16137754347879226367)
XLA Ops:
  0.6 76.9 %shard_map.50 = (f32[64,128,256]{2,1,0:T(8,128)}, f32[64,128,256]{2,1,0:T(8,128)}) custom-call(f32[64,128,256]{2,1,0:T(8,128)} %load_in.1, f32[64,128,256]{2,1,0:T(8,128)} %start_in.1, f32[64,128,256]{2,1,0:T(8,128)} %mass_in.1), custom_call_target="tpu_custom_call" | custom-call | tf_op jit(solution)/shard_map/pallas_call | solution.py:265
  77.5 0.0 copy-start
  77.5 7.9 %copy.7 = f32[64,128,256]{2,1,0:T(8,128)} copy(f32[64,128,256]{2,1,0:T(8,128)} %get-tuple-element.4) | data formatting | bytes 16777216
  85.4 0.0 copy-done
  85.4 3.4 %copy.8 = f32[64,128,256]{2,1,0:T(8,128)} copy(f32[64,128,256]{2,1,0:T(8,128)S(1)} %copy-done) | data formatting | bytes 16777216
Async XLA Ops:
  77.5 7.9 %copy-start = (f32[64,128,256]{2,1,0:T(8,128)S(1)}, f32[64,128,256]{2,1,0:T(8,128)}, u32[]{:S(2)}) copy-start(f32[64,128,256]{2,1,0:T(8,128)} %get-tuple-element.5) | copy-start | bytes 25165828
